TPU v7x, 32 devices: a whole 2x2x4 slice. The times are simulated.
32 devices in a mesh: dp: 4 (over x, core), expert: 8 (over z, y).
Axes of the slice: x: 2, y: 2, z: 4, core: 2. Of those that a mesh axis runs over, the one named last changes fastest.
Arguments:
- tokens: bfloat16 [1024, 6144], P('dp', 'expert'), may hold values from -6 to 6
- cotangent: bfloat16 [1024, 6144], P('dp', 'expert'), may hold values from -6 to 6
- expert_choice: int32 [1024, 2], P('dp'), may hold values from 0 to 3, all different within a row; in each aligned block of 256 rows (0 to 255, 256 to 511, ...) at most 160 rows name the same one
- gate_values: bfloat16 [1024, 2], P('dp'), may hold values from 0.099609375 to 1
- gate_weight: bfloat16 [4, 6144, 2048], P('dp', None, 'expert'), may hold values from -0.078125 to 0.078125
- up_weight: bfloat16 [4, 6144, 2048], P('dp', None, 'expert'), may hold values from -0.078125 to 0.078125
- down_weight: bfloat16 [4, 2048, 6144], P('dp', 'expert'), may hold values from -0.125 to 0.125
- shrinker: bfloat16 [4, 32, 6144], P('dp'), may hold values from -0.078125 to 0.078125
- widener: bfloat16 [4, 2, 16, 2048], P('dp', None, None, 'expert'), may hold values from -0.375 to 0.375
- squeezer: bfloat16 [4, 16, 2048], P('dp', None, 'expert'), may hold values from -0.125 to 0.125
- spreader: bfloat16 [4, 16, 6144], P('dp'), may hold values from -0.375 to 0.375
Outputs:
- token_grad: bfloat16 [1024, 6144], P('dp', 'expert')
- gate_grad: float32 [1024, 2], P('dp')
- shrinker_grad: float32 [4, 32, 6144], P('dp')
- widener_grad: float32 [4, 2, 16, 2048], P('dp', None, None, 'expert')
- squeezer_grad: float32 [4, 16, 2048], P('dp', None, 'expert')
- spreader_grad: float32 [4, 16, 6144], P('dp')
Inputs may be any that keep to these rules, and one draw needn't show every extreme that they name: `expert_choice`: each row names 2 different experts. Among the 256 tokens of one index of dp no expert is chosen more than 160 times, and some expert is chosen exactly 160 times by the tokens of some or all indices of dp.
All inputs are finite; a program needn't handle non-finite values.
Results may differ from a plain program's by a relative error of at most 0.02.
Values may be sent and summed in bfloat16 or wider, within the bound.
A program may use at most 128 MiB of HBM per device.

v0:
```python
import jax
import jax.numpy as jnp
from jax import lax
from jax.sharding import PartitionSpec as P

adapter_scale = 2.0


def product(pattern, operand_a, operand_b):
    return jnp.einsum(pattern, operand_a, operand_b, preferred_element_type=jnp.float32)


def silu_pair(gate_pre):
    logistic = jax.nn.sigmoid(gate_pre)
    return (gate_pre * logistic, logistic * (1.0 + gate_pre * (1.0 - logistic)))


def full_rows(gathered, capacity, part_width):
    n_groups = gathered.shape[0]
    n_sources = gathered.shape[1]
    ordered = gathered.reshape(n_groups, n_sources, capacity, part_width).transpose(1, 2, 0, 3)
    return ordered.reshape(n_sources * capacity, n_groups * part_width)


def local(
    tokens,
    cotangent,
    expert_choice,
    gate_values,
    gate_weight,
    up_weight,
    down_weight,
    shrinker,
    widener,
    squeezer,
    spreader,
):
    tok_rows, part_width = tokens.shape
    top_k = expert_choice.shape[1]
    low_rank = spreader.shape[1]
    n_groups = lax.axis_size("expert")
    n_experts = lax.axis_size("dp")
    capacity = tok_rows * top_k * 5 // (4 * n_experts)
    own_rows = n_experts * capacity
    flat_choice = expert_choice.reshape(-1)
    onehot = (flat_choice[:, None] == jnp.arange(n_experts, dtype=jnp.int32)[None, :]).astype(
        jnp.int32
    )
    before = jnp.cumsum(onehot, axis=0) - onehot
    slot_index = jnp.sum(before * onehot, axis=1)
    target = flat_choice * capacity + slot_index
    placing = target[None, :] == jnp.arange(own_rows, dtype=jnp.int32)[:, None]
    stacked = jnp.repeat(jnp.concatenate([tokens, cotangent], axis=1), top_k, axis=0)
    placed = jnp.dot(
        placing.astype(jnp.bfloat16), stacked, preferred_element_type=jnp.float32
    ).astype(jnp.bfloat16)
    send_x = placed[:, :part_width].reshape(n_experts, capacity * part_width)
    send_dy = placed[:, part_width:].reshape(n_experts, capacity * part_width)
    gate_flat = gate_values.reshape(-1).astype(jnp.float32)
    send_gate = (
        jnp.sum(jnp.where(placing, gate_flat[None, :], 0.0), axis=1)
        .astype(jnp.bfloat16)
        .reshape(n_experts, capacity)
    )
    recv_x, recv_dy, recv_gate = (
        lax.all_to_all(send_x, "dp", split_axis=0, concat_axis=0, tiled=True),
        lax.all_to_all(send_dy, "dp", split_axis=0, concat_axis=0, tiled=True),
        lax.all_to_all(send_gate, "dp", split_axis=0, concat_axis=0, tiled=True),
    )
    gate_rows = recv_gate.reshape(-1).astype(jnp.float32)
    gathered_x = lax.all_gather(recv_x[None], "expert", axis=0, tiled=True)
    rows_x = full_rows(gathered_x, capacity, part_width)
    shrink_local = shrinker[0]
    widen_local = widener[0]
    squeeze_local = squeezer[0]
    spread_local = spreader[0]
    lowrank_in = product("nd,rd->nr", rows_x, shrink_local).astype(jnp.bfloat16)
    gate_pre = jnp.dot(
        rows_x, gate_weight[0], preferred_element_type=jnp.float32
    ) + adapter_scale * jnp.dot(
        lowrank_in[:, :low_rank], widen_local[0], preferred_element_type=jnp.float32
    )
    up_pre = jnp.dot(
        rows_x, up_weight[0], preferred_element_type=jnp.float32
    ) + adapter_scale * jnp.dot(
        lowrank_in[:, low_rank:], widen_local[1], preferred_element_type=jnp.float32
    )
    silu_gate, silu_slope = silu_pair(gate_pre)
    activation = (silu_gate * up_pre).astype(jnp.bfloat16)
    out_part = product("rf,nf->rn", squeeze_local, activation)
    out_low = lax.psum(out_part.astype(jnp.bfloat16), "expert").astype(jnp.float32)
    gathered_dy = lax.all_gather(recv_dy[None], "expert", axis=0, tiled=True)
    rows_dy = full_rows(gathered_dy, capacity, part_width)
    back_down = product("nd,fd->nf", rows_dy, down_weight[0])
    back_low = product("rd,nd->rn", spread_local, rows_dy)
    gate_part = jnp.sum(activation.astype(jnp.float32) * back_down, axis=1)
    scaled_low = (back_low * gate_rows[None, :]).astype(jnp.bfloat16)
    act_delta = gate_rows[:, None] * back_down + adapter_scale * product(
        "rn,rf->nf", scaled_low, squeeze_local
    )
    gate_delta = (act_delta * up_pre * silu_slope).astype(jnp.bfloat16)
    up_delta = (act_delta * silu_gate).astype(jnp.bfloat16)
    back_part = jnp.concatenate(
        [
            product("rf,nf->rn", widen_local[0], gate_delta),
            product("rf,nf->rn", widen_local[1], up_delta),
        ],
        axis=0,
    )
    back_sum, gate_sum = (
        lax.psum(back_part.astype(jnp.bfloat16), "expert").astype(jnp.float32),
        lax.psum(gate_part.astype(jnp.bfloat16), "expert").astype(jnp.float32),
    )
    low_out = out_low.astype(jnp.bfloat16)
    gate_dots = gate_sum + adapter_scale * jnp.sum(low_out.astype(jnp.float32) * back_low, axis=0)
    back_in = back_sum.astype(jnp.bfloat16)
    gate_blocks = gate_weight[0].reshape(n_groups, part_width, gate_weight.shape[2])
    up_blocks = up_weight[0].reshape(n_groups, part_width, up_weight.shape[2])
    term = product("nf,kdf->knd", gate_delta, gate_blocks) + product(
        "nf,kdf->knd", up_delta, up_blocks
    )
    token_part = (
        lax.psum_scatter(
            term.reshape(1 * lax.axis_size("expert"), own_rows * part_width).astype(jnp.bfloat16),
            "expert",
            scatter_dimension=0,
            tiled=True,
        )
        .astype(jnp.float32)
        .reshape(own_rows, part_width)
    )
    shrink_cols = lax.dynamic_slice_in_dim(
        shrink_local, lax.axis_index("expert") * part_width, part_width, 1
    )
    token_part = token_part + adapter_scale * product("rn,rd->nd", back_in, shrink_cols)
    token_back, gate_back = (
        lax.all_to_all(
            token_part.reshape(n_experts, capacity * part_width).astype(jnp.bfloat16),
            "dp",
            split_axis=0,
            concat_axis=0,
            tiled=True,
        ).astype(jnp.float32),
        lax.all_to_all(
            gate_dots.reshape(n_experts, capacity).astype(jnp.bfloat16),
            "dp",
            split_axis=0,
            concat_axis=0,
            tiled=True,
        ).astype(jnp.float32),
    )
    picked = jnp.take(token_back.reshape(own_rows, part_width), target, axis=0)
    token_grad = jnp.sum(picked.reshape(tok_rows, top_k, part_width), axis=1).astype(jnp.bfloat16)
    gate_grad = jnp.take(gate_back.reshape(own_rows), target).reshape(tok_rows, top_k)
    shrinker_grad = adapter_scale * product("rn,nd->rd", back_in, rows_x)
    widener_grad = adapter_scale * jnp.stack(
        [
            product("nr,nf->rf", lowrank_in[:, :low_rank], gate_delta),
            product("nr,nf->rf", lowrank_in[:, low_rank:], up_delta),
        ]
    )
    squeezer_grad = adapter_scale * product("rn,nf->rf", scaled_low, activation)
    weighted_low = (out_low * gate_rows[None, :]).astype(jnp.bfloat16)
    spreader_grad = adapter_scale * product("rn,nd->rd", weighted_low, rows_dy)
    return (
        token_grad,
        gate_grad,
        shrinker_grad[None],
        widener_grad[None],
        squeezer_grad[None],
        spreader_grad[None],
    )


def solution(mesh):
    placed = (
        P("dp", "expert"),
        P("dp", "expert"),
        P("dp", None),
        P("dp", None),
        P("dp", None, "expert"),
        P("dp", None, "expert"),
        P("dp", "expert", None),
        P("dp", None, None),
        P("dp", None, None, "expert"),
        P("dp", None, "expert"),
        P("dp", None, None),
    )
    return jax.shard_map(
        local,
        mesh=mesh,
        in_specs=placed,
        out_specs=(
            P("dp", "expert"),
            P("dp", None),
            P("dp", None, None),
            P("dp", None, None, "expert"),
            P("dp", None, "expert"),
            P("dp", None, None),
        ),
        check_vma=False,
    )
```

profile of v0, /device:TPU:5, one launch (start us, length us, event | category | flops | bytes accessed | tf_op | source)
XLA Modules:
  0.0 962.6 jit_solution(5538377547508068036)
XLA Ops:
  13.4 4.6 reshape.230
  22.0 3.6 all_to_all.31
  26.2 9.3 reduce.14
  35.6 3.1 reshape.284
  38.7 18.2 %all_to_all.38 = bf16[4,2,61440]{2,1,0:T(2,128)(2,1)} all-to-all(bf16[4,2,61440]{2,1,0:T(2,128)(2,1)} %reshape.284), channel_id=1, replica_groups=mesh['dp'=4,'expert'=8] {'dp'}, dimensions={0} | all-to-all | bytes 1966080 | tf_op jit(solution)/shard_map/all_to_all | solution.py:67
  56.9 3.9 reshape.285
  60.9 3.7 all_to_all.32
  64.5 9.3 reduce.15
  73.9 3.2 reshape.282
  77.1 18.3 %all_to_all.39 = bf16[4,2,61440]{2,1,0:T(2,128)(2,1)} all-to-all(bf16[4,2,61440]{2,1,0:T(2,128)(2,1)} %reshape.282), channel_id=1, replica_groups=mesh['dp'=4,'expert'=8] {'dp'}, dimensions={0} | all-to-all | bytes 1966080 | tf_op jit(solution)/shard_map/all_to_all | solution.py:66
  95.4 3.9 reshape.283
  100.0 6.4 all_to_all.40
  106.5 167.7 %all-gather.5.cloned.1.call-done = bf16[32,1,122880]{2,1,0:T(2,128)(2,1)} async-done(((bf16[4,1,122880]{2,1,0:T(2,128)(2,1)}), bf16[32,1,122880]{2,1,0:T(2,128)(2,1)}) %all-gather.5.cloned.1.call-update) | async-done | bytes 7864336 | tf_op jit(solution)/shard_map/all_gather | solution.py:92
  274.2 48.0 %reduce.2 = bf16[32,122880]{1,0:T(8,128)(2,1)} reduce(bf16[32,1,122880]{2,1,0:T(2,128)(2,1)} %all-gather.5.cloned.1.call-done, bf16[]{:T(256)} %constant.69), dimensions={1}, to_apply=%all-gather.reduce_sub_computation | reduce | bytes 15728642 | tf_op jit(solution)/shard_map/all_gather | solution.py:92
  322.2 8.2 copy.75
  330.4 10.9 %copy.60 = bf16[4,160,8,768]{3,2,1,0:T(8,128)(2,1)} copy(bf16[4,160,8,768]{3,1,0,2:T(8,128)(2,1)} %bitcast.132) | data formatting | bytes 15728640 | tf_op jit(solution)/shard_map/transpose | solution.py:21
  341.2 9.1 copy.76
  350.3 5.5 convolution_bitcast_fusion
  355.8 3.7 fusion.7
  359.5 129.5 %all-gather.7.cloned.1.call-done = bf16[32,1,122880]{2,1,0:T(2,128)(2,1)} async-done(((bf16[4,1,122880]{2,1,0:T(2,128)(2,1)}), bf16[32,1,122880]{2,1,0:T(2,128)(2,1)}) %all-gather.7.cloned.1.call-update) | async-done | bytes 7864336 | tf_op jit(solution)/shard_map/all_gather | solution.py:71
  489.0 47.5 %reduce.3 = bf16[32,122880]{1,0:T(8,128)(2,1)} reduce(bf16[32,1,122880]{2,1,0:T(2,128)(2,1)} %all-gather.7.cloned.1.call-done, bf16[]{:T(256)} %constant.69), dimensions={1}, to_apply=%all-gather.1.reduce_sub_computation | reduce | bytes 15728642 | tf_op jit(solution)/shard_map/all_gather | solution.py:71
  536.5 8.2 copy.77
  544.7 10.8 %copy.63 = bf16[4,160,8,768]{3,2,1,0:T(8,128)(2,1)} copy(bf16[4,160,8,768]{3,1,0,2:T(8,128)(2,1)} %bitcast.134) | data formatting | bytes 15728640 | tf_op jit(solution)/shard_map/transpose | solution.py:21
  555.5 8.9 copy.78
  564.4 5.8 convolution_convert_fusion.1
  570.2 3.3 fusion.3
  573.6 2.9 fusion.5
  579.0 7.8 fusion.21
  586.8 11.1 %fusion.2 = bf16[1,8,640,768]{3,2,1,0:T(8,128)(2,1)} fusion(f32[640,8,768]{2,0,1:T(8,128)} %fusion.21, bf16[8,768,256]{2,1,0:T(8,128)(2,1)S(1)} %bitcast.136, bf16[640,256]{0,1:T(8,128)(2,1)S(1)} %get-tuple-element.40), kind=kOutput, calls=%fused_computation.7 | convolution fusion | flops 2021130240 | bytes 27066368 | tf_op jit(solution)/shard_map/nf,kdf->knd/dot_general | solution.py:10
  597.9 10.9 %copy.79 = bf16[1,8,640,768]{3,1,2,0:T(8,128)(2,1)} copy(bf16[1,8,640,768]{3,2,1,0:T(8,128)(2,1)} %fusion.2) | data formatting | bytes 15728640
  616.6 31.5 %all-reduce.1 = (bf16[32,640]{1,0:T(8,128)(2,1)S(1)}, bf16[16,640]{1,0:T(8,128)(2,1)S(1)}, bf16[640]{0:T(1024)(128)(2,1)}) all-reduce(bf16[32,640]{1,0:T(8,128)(2,1)} %pad_maximum_fusion.1, bf16[16,640]{1,0:T(8,128)(2,1)} %fusion.15, bf16[640]{0:T(1024)(128)(2,1)} %get-tuple-element.35), channel_id=1, replica_groups=mesh['dp'=4,'expert'=8] {'expert'}, use_global_device_ids=true, to_apply=%region_5.6 | all-reduce | flops 31360 | bytes 125440 | tf_op jit(solution)/shard_map/psum | solution.py:111
  650.8 8.5 all-to-all-start.4
  664.1 5.7 fusion
  669.7 195.0 %all-reduce.4.cloned.1.call-done = bf16[8,491520]{1,0:T(8,128)(2,1)} async-done(((bf16[8,491520]{1,0:T(8,128)(2,1)}), bf16[8,491520]{1,0:T(8,128)(2,1)}) %all-reduce.4.cloned.1.call-update) | async-done | bytes 7864336
  864.8 21.8 %fusion.9 = f32[491520]{0:T(1024)} fusion(bf16[8,491520]{1,0:T(8,128)(2,1)} %all-reduce.4.cloned.1.call-done, u32[]{:T(128)} %bitcast.28), kind=kLoop, calls=%fused_computation.16 | loop fusion | flops 491520 | bytes 2949124 | tf_op jit(solution)/shard_map/reshape | solution.py:130
  886.6 2.7 reshape.240
  889.3 3.0 add_convert_fusion.1
  892.3 3.8 convert_element_type.181
  896.1 9.3 reduce.16
  905.4 3.1 reshape.286
  908.6 5.3 all-to-all-start.3
  913.9 5.1 fusion.1
  926.7 3.9 reshape.287
  930.6 8.9 convert_reduce_fusion
  939.5 4.2 reshape.241
  943.7 4.7 gather_fusion
  948.4 3.0 gather.13
  951.5 4.2 select_reduce_fusion
  (85 shorter events, 37.0 us)
Async XLA Ops:
  7.2 563.0 %copy-start = (bf16[1,6144,256]{2,1,0:T(8,128)(2,1)S(1)}, bf16[1,6144,256]{2,1,0:T(8,128)(2,1)}, u32[]{:S(2)}) copy-start(bf16[1,6144,256]{2,1,0:T(8,128)(2,1)} %param.15) | copy-start | bytes 9437188
  7.2 267.0 %all-gather.5.cloned.1.call-start = ((), (), s32[]{:S(2)}) async-start(), calls=%async_computation.5 | async-start | bytes 17694720 | tf_op jit(solution)/shard_map/all_gather | solution.py:92
  60.8 428.2 %all-gather.7.cloned.1.call-start = ((), (), s32[]{:S(2)}) async-start(), calls=%async_computation.6 | async-start | bytes 17694720 | tf_op jit(solution)/shard_map/all_gather | solution.py:71
  77.1 22.3 %copy-start.12 = (bf16[256,2]{0,1:T(2,128)(2,1)S(1)}, bf16[256,2]{0,1:T(2,128)(2,1)}, u32[]{:S(2)}) copy-start(bf16[256,2]{0,1:T(2,128)(2,1)} %param.14) | copy-start | bytes 3076
  99.3 765.5 %all-reduce.4.cloned.1.call-start = ((), (), s32[]{:S(2)}) async-start(), calls=%async_computation.7 | async-start | bytes 15728640
  341.2 9.1 copy-start.8
  341.2 14.6 %copy-start.13 = (bf16[1,256,6144]{2,1,0:T(8,128)(2,1)S(1)}, bf16[1,256,6144]{2,1,0:T(8,128)(2,1)}, u32[]{:S(2)}) copy-start(bf16[1,256,6144]{2,1,0:T(8,128)(2,1)} %param.17) | copy-start | bytes 9437188
  350.3 5.5 copy-start.1
  555.5 8.9 copy-start.7
  564.4 5.8 copy-start.2
  570.2 3.3 copy-start.3
  573.5 3.0 copy-start.9
  573.5 3.3 copy-start.6
  573.5 3.3 copy-start.10
  579.0 7.8 copy-start.4
  579.0 7.8 copy-start.5
  608.8 1.9 copy-start.14
  650.8 257.8 %all-to-all-start.4 = ((bf16[4,1,160]{2,1,0:T(2,128)(2,1)}), bf16[4,1,160]{2,1,0:T(2,128)(2,1)}, u32[]{:S(2)}, u32[]{:S(2)}) async-start(bf16[4,1,160]{2,1,0:T(2,128)(2,1)} %convert_element_type.182), calls=%async_computation.4 | async-start | bytes 8192 | tf_op jit(solution)/shard_map/all_to_all | solution.py:144
  908.6 18.1 %all-to-all-start.3 = ((bf16[4,2,61440]{2,1,0:T(2,128)(2,1)}), bf16[4,2,61440]{2,1,0:T(2,128)(2,1)}, u32[]{:S(2)}, u32[]{:S(2)}) async-start(bf16[4,2,61440]{2,1,0:T(2,128)(2,1)} %reshape.286), calls=%async_computation.3 | async-start | bytes 1966080 | tf_op jit(solution)/shard_map/all_to_all | solution.py:137
  913.9 5.9 copy-start.11
Sparse Core Ops, SparseCore 0:
  60.9 213.1 all-gather.4
  276.4 212.6 all-gather.6
  608.9 255.7 all-reduce.3
where the time goes:
time: 975 us; the launch traced here: 963 us
  waiting for transfers between devices  493 us (51%)
  other arithmetic  167 us (17%)
  local copies, waits for them, and re-layouts  132 us (14%)
  blocking collectives  74.3 us (8%)
  matrix products  67.2 us (7%)
  between operations  14.5 us (1%)
  starting transfers between devices  13.9 us (1%)
    unnamed x4, waiting for transfers between devices  195 us
    all_gather x1, waiting for transfers between devices, local(): gathered_dy = lax.all_gather(recv_dy[None], 'expert', axis=0, tiled=True)  168 us
    all_gather x1, waiting for transfers between devices, local(): gathered_x = lax.all_gather(recv_x[None], 'expert', axis=0, tiled=True)  130 us
    unnamed x44, local copies, waits for them, and re-layouts  69.7 us
    dot_general x15, matrix products, product(): jnp.einsum(pattern, operand_a, operand_b, preferred_element_type=jnp.floa...  56.2 us
    all_gather x1, other arithmetic, local(): gathered_dy = lax.all_gather(recv_dy[None], 'expert', axis=0, tiled=True)  48 us
    all_gather x1, other arithmetic, local(): gathered_x = lax.all_gather(recv_x[None], 'expert', axis=0, tiled=True)  47.5 us
    psum x1, blocking collectives, local(): lax.psum(back_part.astype(jnp.bfloat16), 'expert').astype(jnp.float32)  31.5 us
  transfers between devices with their start and end apart: 5, of which 4 were waited for; matrix products, arithmetic and copies ran while one was open for 19% of the time, Pallas kernels for 0%

commit v1 on v0

v1 whole, which is shorter than its diff:
```python
import functools

import jax
import jax.numpy as jnp
from jax import lax
from jax.experimental import pallas as pl
from jax.experimental.pallas import tpu as pltpu
from jax.sharding import PartitionSpec as P

adapter_scale = 2.0
MESH = pl.DeviceIdType.MESH
tile_rows = 16


def product(pattern, operand_a, operand_b):
    return jnp.einsum(pattern, operand_a, operand_b, preferred_element_type=jnp.float32)


def silu_pair(gate_pre):
    logistic = jax.nn.sigmoid(gate_pre)
    return (gate_pre * logistic, logistic * (1.0 + gate_pre * (1.0 - logistic)))


def grid_of(n):
    inner = 1 << ((n.bit_length() - 1) // 2)
    return n // inner, inner


def ring_position(index, n):
    outer, inner = grid_of(n)
    span = inner - 1
    z, y = lax.div(index, inner), lax.rem(index, inner)
    odd = lax.rem(z, 2)
    walk = z * span + (1 - odd) * (y - 1) + odd * (span - y)
    back = outer * span + outer - 1 - z
    inside = lax.div(y + inner - 1, inner)
    return inside * walk + (1 - inside) * back


def ring_index(position, n):
    outer, inner = grid_of(n)
    span = inner - 1
    returning = lax.div(position, outer * span)
    z = lax.div(position, span)
    step = lax.rem(position, span)
    odd = lax.rem(z, 2)
    walk = z * inner + (1 - odd) * (1 + step) + odd * (span - step)
    back = (outer - 1 - (position - outer * span)) * inner
    return (1 - returning) * walk + returning * back


def meet(me_dp, me_ex, n_dp, left, right):
    barrier = pltpu.get_barrier_semaphore()
    for other in (left, right):
        pl.semaphore_signal(barrier, inc=1, device_id=(me_dp, other), device_id_type=MESH)
    for k in range(1, n_dp):
        peer = lax.rem(me_dp + k, n_dp)
        pl.semaphore_signal(barrier, inc=1, device_id=(peer, me_ex), device_id_type=MESH)
    pl.semaphore_wait(barrier, 2 + n_dp - 1)


def block_view(ref, row, rows, group, width, wide):
    rows_at = pl.ds(pl.multiple_of(row, tile_rows), rows)
    if wide:
        return ref.at[rows_at, pl.ds(pl.multiple_of(group * width, 128), width)]
    return ref.at[group, rows_at]


def gather_kernel(n, n_dp, cap, width, wide, x_ref, dy_ref, gate_ref, ox, ody, ogate,
                  local_sem, sent, came, ring_sent, ring_came):
    me_dp, me_ex = lax.axis_index("dp"), lax.axis_index("expert")
    here = ring_position(me_ex, n)
    around = [ring_index(lax.rem(here + j, n), n) for j in range(n)]
    right, left = around[1], around[n - 1]
    meet(me_dp, me_ex, n_dp, left, right)
    sources, outs = (x_ref, dy_ref), (ox, ody)

    def remote(src, dst, send_sem, recv_sem, dp, ex):
        return pltpu.make_async_remote_copy(
            src_ref=src, dst_ref=dst, send_sem=send_sem, recv_sem=recv_sem,
            device_id=(dp, ex), device_id_type=MESH)

    local, first, pending = [], {}, []
    for k in range(1, n_dp):
        peer = lax.rem(me_dp + k, n_dp)
        copy = remote(gate_ref.at[peer], ogate.at[me_dp], sent.at[2, k], came.at[2, k], peer, me_ex)
        copy.start()
        pending.append(copy)
    copy = pltpu.make_async_copy(gate_ref.at[me_dp], ogate.at[me_dp], local_sem.at[2])
    copy.start()
    local.append(copy)
    for a in range(2):
        for k in range(n_dp):
            peer = lax.rem(me_dp + k, n_dp)
            src = sources[a].at[pl.ds(pl.multiple_of(peer * cap, tile_rows), cap)]
            dst = block_view(outs[a], me_dp * cap, cap, me_ex, width, wide)
            if k == 0:
                copy = pltpu.make_async_copy(src, dst, local_sem.at[a])
            else:
                copy = remote(src, dst, sent.at[a, k], came.at[a, k], peer, me_ex)
            copy.start()
            first[a, k] = copy
    last = {}
    for s in range(n - 1):
        for a in range(2):
            for k in range(n_dp):
                if s > 0:
                    last[a, k].wait_recv()
                elif k > 0:
                    first[a, k].wait_recv()
                else:
                    first[a, k].wait()
                row = lax.rem(me_dp + n_dp - k, n_dp) * cap
                forward = k % 2 == 0
                group = around[(n - s) % n] if forward else around[s]
                view = block_view(outs[a], row, cap, group, width, wide)
                copy = remote(view, view, ring_sent.at[s, a, k], ring_came.at[s, a, k],
                              me_dp, right if forward else left)
                copy.start()
                last[a, k] = copy
                pending.append(copy)
    for a in range(2):
        for k in range(n_dp):
            last[a, k].wait_recv()
            if k > 0:
                first[a, k].wait_send()
    for copy in pending[:n_dp - 1]:
        copy.wait_recv()
    for copy in pending:
        copy.wait_send()
    local[0].wait()


def scatter_kernel(n, n_dp, cap, width, wide, term, extra, gate_ref, back, ogate,
                   slots, final, local_sem, sent, came, ring_sent, ring_came):
    me_dp, me_ex = lax.axis_index("dp"), lax.axis_index("expert")
    here = ring_position(me_ex, n)
    around = [ring_index(lax.rem(here + j, n), n) for j in range(n)]
    right, left = around[1], around[n - 1]
    meet(me_dp, me_ex, n_dp, left, right)

    def remote(src, dst, send_sem, recv_sem, dp, ex):
        return pltpu.make_async_remote_copy(
            src_ref=src, dst_ref=dst, send_sem=send_sem, recv_sem=recv_sem,
            device_id=(dp, ex), device_id_type=MESH)

    def own_part(row, group):
        at = pl.ds(pl.multiple_of(row, tile_rows), tile_rows)
        if wide:
            return term[at, pl.ds(pl.multiple_of(group * width, 128), width)].astype(jnp.float32)
        return term[group, at].astype(jnp.float32)

    pending, arrivals = [], []
    for k in range(1, n_dp):
        peer = lax.rem(me_dp + k, n_dp)
        copy = remote(gate_ref.at[peer], ogate.at[me_dp], sent.at[1, k], came.at[1, k], peer, me_ex)
        copy.start()
        pending.append(copy)
        arrivals.append(copy)
    own_gate = pltpu.make_async_copy(gate_ref.at[me_dp], ogate.at[me_dp], local_sem.at[1])
    own_gate.start()
    last = {}
    for s in range(n - 1):
        for k in range(n_dp):
            row = lax.rem(me_dp + k, n_dp) * cap
            rows_at = pl.ds(pl.multiple_of(row, tile_rows), cap)
            forward = k % 2 == 0
            group = around[(n - 1 - s) % n] if forward else around[(1 + s) % n]
            if s == 0:
                src = block_view(term, row, cap, group, width, wide)
            else:
                last[k].wait_recv()
                src = slots.at[s - 1, rows_at]

                def add(i, carry, row=row, group=group, s=s):
                    start = row + i * tile_rows
                    at = pl.ds(pl.multiple_of(start, tile_rows), tile_rows)
                    total = slots[s - 1, at].astype(jnp.float32) + own_part(start, group)
                    slots[s - 1, at] = total.astype(jnp.bfloat16)
                    return carry

                lax.fori_loop(0, cap // tile_rows, add, 0)
            copy = remote(src, slots.at[s, rows_at], ring_sent.at[s, k], ring_came.at[s, k],
                          me_dp, right if forward else left)
            copy.start()
            last[k] = copy
            pending.append(copy)
    own_rows = None
    for k in list(range(1, n_dp)) + [0]:
        peer = lax.rem(me_dp + k, n_dp)
        row = peer * cap
        last[k].wait_recv()

        def finish(i, carry, row=row):
            start = row + i * tile_rows
            at = pl.ds(pl.multiple_of(start, tile_rows), tile_rows)
            total = slots[n - 2, at].astype(jnp.float32) + own_part(start, me_ex) + extra[at]
            final[at] = total.astype(jnp.bfloat16)
            return carry

        lax.fori_loop(0, cap // tile_rows, finish, 0)
        src = final.at[pl.ds(pl.multiple_of(row, tile_rows), cap)]
        dst = back.at[pl.ds(pl.multiple_of(me_dp * cap, tile_rows), cap)]
        if k == 0:
            own_rows = pltpu.make_async_copy(src, dst, local_sem.at[0])
            own_rows.start()
        else:
            copy = remote(src, dst, sent.at[0, k], came.at[0, k], peer, me_ex)
            copy.start()
            pending.append(copy)
            arrivals.append(copy)
    for copy in arrivals:
        copy.wait_recv()
    for copy in pending:
        copy.wait_send()
    own_gate.wait()
    own_rows.wait()


def spread_rows(values, n_dp, cap):
    lanes = -(-cap // 128) * 128
    padded = jnp.pad(values.reshape(n_dp, 1, cap), ((0, 0), (0, 0), (0, lanes - cap)))
    return jnp.broadcast_to(padded, (n_dp, tile_rows, lanes)).astype(jnp.bfloat16)


def local(
    tokens,
    cotangent,
    expert_choice,
    gate_values,
    gate_weight,
    up_weight,
    down_weight,
    shrinker,
    widener,
    squeezer,
    spreader,
):
    tok_rows, width = tokens.shape
    top_k = expert_choice.shape[1]
    low_rank = spreader.shape[1]
    n = lax.axis_size("expert")
    n_dp = lax.axis_size("dp")
    cap = tok_rows * top_k * 5 // (4 * n_dp)
    own_rows = n_dp * cap
    wide = width % 128 == 0
    bf16, f32 = jnp.bfloat16, jnp.float32
    vmem = pl.BlockSpec(memory_space=pltpu.VMEM)
    anywhere = pl.BlockSpec(memory_space=pl.ANY)
    dma = pltpu.SemaphoreType.DMA

    flat_choice = expert_choice.reshape(-1)
    onehot = (flat_choice[:, None] == jnp.arange(n_dp, dtype=jnp.int32)[None, :]).astype(jnp.int32)
    before = jnp.cumsum(onehot, axis=0) - onehot
    slot_index = jnp.sum(before * onehot, axis=1)
    target = (flat_choice * cap + slot_index).reshape(tok_rows, top_k)
    row_ids = jnp.arange(own_rows, dtype=jnp.int32)
    hits = [target[None, :, k] == row_ids[:, None] for k in range(top_k)]
    placing = functools.reduce(jnp.logical_or, hits).astype(bf16)
    send_x = jnp.dot(placing, tokens, preferred_element_type=f32).astype(bf16)
    send_dy = jnp.dot(placing, cotangent, preferred_element_type=f32).astype(bf16)
    gates = gate_values.astype(f32)
    send_gate = sum(
        jnp.sum(jnp.where(hits[k], gates[None, :, k], 0.0), axis=1) for k in range(top_k)
    )
    gate_block = spread_rows(send_gate, n_dp, cap)
    whole = (own_rows, n * width) if wide else (n, own_rows, width)
    rows_x, rows_dy, gate_all = pl.pallas_call(
        functools.partial(gather_kernel, n, n_dp, cap, width, wide),
        out_shape=(
            jax.ShapeDtypeStruct(whole, bf16),
            jax.ShapeDtypeStruct(whole, bf16),
            jax.ShapeDtypeStruct(gate_block.shape, bf16),
        ),
        in_specs=[vmem] * 3,
        out_specs=(anywhere,) * 3,
        scratch_shapes=[
            dma((3,)),
            dma((3, n_dp)),
            dma((3, n_dp)),
            dma((n - 1, 2, n_dp)),
            dma((n - 1, 2, n_dp)),
        ],
        compiler_params=pltpu.CompilerParams(collective_id=0, has_side_effects=True),
    )(send_x, send_dy, gate_block)
    if not wide:
        rows_x = rows_x.transpose(1, 0, 2).reshape(own_rows, n * width)
        rows_dy = rows_dy.transpose(1, 0, 2).reshape(own_rows, n * width)
    gate_rows = gate_all[:, 0, :cap].reshape(-1).astype(f32)

    shrink_local = shrinker[0]
    widen_local = widener[0]
    squeeze_local = squeezer[0]
    spread_local = spreader[0]
    lowrank_in = product("nd,rd->nr", rows_x, shrink_local).astype(bf16)
    gate_pre = jnp.dot(
        rows_x, gate_weight[0], preferred_element_type=f32
    ) + adapter_scale * jnp.dot(
        lowrank_in[:, :low_rank], widen_local[0], preferred_element_type=f32
    )
    up_pre = jnp.dot(
        rows_x, up_weight[0], preferred_element_type=f32
    ) + adapter_scale * jnp.dot(
        lowrank_in[:, low_rank:], widen_local[1], preferred_element_type=f32
    )
    silu_gate, silu_slope = silu_pair(gate_pre)
    activation = (silu_gate * up_pre).astype(bf16)
    out_part = product("rf,nf->rn", squeeze_local, activation)
    back_down = product("nd,fd->nf", rows_dy, down_weight[0])
    back_low = product("rd,nd->rn", spread_local, rows_dy)
    gate_part = jnp.sum(activation.astype(f32) * back_down, axis=1)
    scaled_low = (back_low * gate_rows[None, :]).astype(bf16)
    act_delta = gate_rows[:, None] * back_down + adapter_scale * product(
        "rn,rf->nf", scaled_low, squeeze_local
    )
    gate_delta = (act_delta * up_pre * silu_slope).astype(bf16)
    up_delta = (act_delta * silu_gate).astype(bf16)
    parts = jnp.concatenate(
        [
            out_part,
            product("rf,nf->rn", widen_local[0], gate_delta),
            product("rf,nf->rn", widen_local[1], up_delta),
            gate_part[None],
        ],
        axis=0,
    ).astype(bf16)
    sums = lax.psum(parts, "expert")
    low_out = sums[:low_rank]
    out_low = low_out.astype(f32)
    back_in = sums[low_rank : 3 * low_rank]
    gate_dots = sums[3 * low_rank].astype(f32) + adapter_scale * jnp.sum(out_low * back_low, axis=0)
    term = (
        product("nf,df->nd", gate_delta, gate_weight[0])
        + product("nf,df->nd", up_delta, up_weight[0])
    ).astype(bf16)
    if not wide:
        term = term.reshape(own_rows, n, width).transpose(1, 0, 2)
    shrink_cols = lax.dynamic_slice_in_dim(
        shrink_local, lax.axis_index("expert") * width, width, 1
    )
    extra = adapter_scale * product("rn,rd->nd", back_in, shrink_cols)
    token_back, gate_back = pl.pallas_call(
        functools.partial(scatter_kernel, n, n_dp, cap, width, wide),
        out_shape=(
            jax.ShapeDtypeStruct((own_rows, width), bf16),
            jax.ShapeDtypeStruct(gate_block.shape, bf16),
        ),
        in_specs=[vmem] * 3,
        out_specs=(anywhere,) * 2,
        scratch_shapes=[
            pltpu.VMEM((n - 1, own_rows, width), bf16),
            pltpu.VMEM((own_rows, width), bf16),
            dma((2,)),
            dma((2, n_dp)),
            dma((2, n_dp)),
            dma((n - 1, n_dp)),
            dma((n - 1, n_dp)),
        ],
        compiler_params=pltpu.CompilerParams(
            collective_id=1, has_side_effects=True, vmem_limit_bytes=40 * 1024 * 1024
        ),
    )(term, extra, spread_rows(gate_dots, n_dp, cap))
    token_grad = product("rt,rd->td", placing, token_back).astype(bf16)
    gate_flat = gate_back[:, 0, :cap].reshape(own_rows).astype(f32)
    gate_grad = jnp.stack(
        [jnp.sum(jnp.where(hits[k], gate_flat[:, None], 0.0), axis=0) for k in range(top_k)],
        axis=1,
    )
    shrinker_grad = adapter_scale * product("rn,nd->rd", back_in, rows_x)
    widener_grad = adapter_scale * jnp.stack(
        [
            product("nr,nf->rf", lowrank_in[:, :low_rank], gate_delta),
            product("nr,nf->rf", lowrank_in[:, low_rank:], up_delta),
        ]
    )
    squeezer_grad = adapter_scale * product("rn,nf->rf", scaled_low, activation)
    weighted_low = (out_low * gate_rows[None, :]).astype(bf16)
    spreader_grad = adapter_scale * product("rn,nd->rd", weighted_low, rows_dy)
    return (
        token_grad,
        gate_grad,
        shrinker_grad[None],
        widener_grad[None],
        squeezer_grad[None],
        spreader_grad[None],
    )


def solution(mesh):
    placed = (
        P("dp", "expert"),
        P("dp", "expert"),
        P("dp", None),
        P("dp", None),
        P("dp", None, "expert"),
        P("dp", None, "expert"),
        P("dp", "expert", None),
        P("dp", None, None),
        P("dp", None, None, "expert"),
        P("dp", None, "expert"),
        P("dp", None, None),
    )
    return jax.shard_map(
        local,
        mesh=mesh,
        in_specs=placed,
        out_specs=(
            P("dp", "expert"),
            P("dp", None),
            P("dp", None, None),
            P("dp", None, None, "expert"),
            P("dp", None, "expert"),
            P("dp", None, None),
        ),
        check_vma=False,
    )
```

time: 975 us -> 358 us (0.37); the launches traced: 963 us -> 358 us
  waiting for transfers between devices: 493 us -> 0 us
  Pallas kernels: 0 us -> 257 us
  other arithmetic: 167 us -> 7.31 us
  local copies, waits for them, and re-layouts: 132 us -> 8.91 us
  blocking collectives: 74.3 us -> 26.3 us
  starting transfers between devices: 13.9 us -> 0 us
  between operations: 14.5 us -> 0.96 us
  matrix products: 67.2 us -> 57.1 us
    all_gather x2 -> x0, waiting for transfers between devices: 297 us -> none  [the longest x1 168 us: local(): gathered_dy = lax.all_gather(recv_dy[None], 'expert', axis=0, tiled=True)]
    pallas_call x0 -> x2, Pallas kernels: none -> 257 us  [the longest x1 161 us: local(): pl.pallas_call(functools.partial(gather_kernel, n, n_dp, cap, width, wide...]
    unnamed x4 -> x0, waiting for transfers between devices: 195 us -> none
    all_gather x2 -> x0, other arithmetic: 95.5 us -> none  [the longest x1 48 us: local(): gathered_dy = lax.all_gather(recv_dy[None], 'expert', axis=0, tiled=True)]
    unnamed x44 -> x33, local copies, waits for them, and re-layouts: 69.7 us -> 4.3 us
    all_to_all x3 -> x0, blocking collectives: 42.9 us -> none  [the longest x1 18.3 us: local(): lax.all_to_all(send_x, 'dp', split_axis=0, concat_axis=0, tiled=True)]
    reshape x1 -> x0, other arithmetic: 21.8 us -> none  [local(): token_part = lax.psum_scatter(term.reshape(1 * lax.axis_size('expert'), o...]
    transpose x2 -> x0, local copies, waits for them, and re-layouts: 21.6 us -> none  [full_rows(): gathered.reshape(n_groups, n_sources, capacity, part_width)]
  transfers between devices with their start and end apart: 5 -> 0, of which waited for: 4 -> 0; matrix products, arithmetic and copies ran while one was open for 19% -> 0% of each run, Pallas kernels for 0% -> 0%
where the time goes in v1:
time: 358 us
  Pallas kernels  257 us (72%)
  matrix products  57.1 us (16%)
  blocking collectives  26.3 us (7%)
  local copies, waits for them, and re-layouts  8.91 us (2%)
  other arithmetic  7.31 us (2%)
    pallas_call x1, Pallas kernels, local(): pl.pallas_call(functools.partial(gather_kernel, n, n_dp, cap, width, wide...  161 us
    pallas_call x1, Pallas kernels, local(): pl.pallas_call(functools.partial(scatter_kernel, n, n_dp, cap, width, wid...  96.4 us
    dot_general x16, matrix products, product(): jnp.einsum(pattern, operand_a, operand_b, preferred_element_type=jnp.floa...  45.5 us
    psum x1, blocking collectives, local(): sums = lax.psum(parts, 'expert')  26.3 us

profile of v1, /device:TPU:5, one launch (start us, length us, event | category | flops | bytes accessed | tf_op | source)
XLA Modules:
  0.0 357.7 jit_solution(2807255884055161692)
XLA Ops:
  0.7 0.9 fusion.61
  1.5 1.0 copy.33
  2.5 0.1 eq.59
  2.7 0.1 eq.55
  2.8 1.2 reduce-window.6
  4.0 0.2 slice_reduce_fusion
  4.2 0.2 reduce-window.9
  4.5 0.1 reduce_sum.66
  4.8 0.7 multiply_add_fusion
  5.5 0.2 select_reduce_fusion.2
  5.7 0.1 add.56
  5.8 0.6 broadcast_in_dim.73.gate_ref
  6.5 2.4 convolution_convert_fusion.dy_ref
  8.8 2.4 convolution_convert_fusion.1.x_ref
  11.3 160.8 %shard_map.154 = (bf16[640,6144]{1,0:T(8,128)(2,1)}, bf16[640,6144]{1,0:T(8,128)(2,1)}, bf16[4,16,256]{2,1,0:T(8,128)(2,1)}) custom-call(bf16[640,768]{1,0:T(8,128)(2,1)} %convolution_convert_fusion.1.x_ref, bf16[640,768]{1,0:T(8,128)(2,1)} %convolution_convert_fusion.dy_ref, bf16[4,16,256]{2,1,0:T(8,128)(2,1)} %broadcast_in_dim.73.gate_ref), custom_call_target="tpu_custom_call" | custom-call | tf_op jit(solution)/shard_map/pallas_call | solution.py:268
  172.1 0.7 convert_reduce_fusion.1
  172.9 5.8 %convolution_convert_fusion.3 = bf16[640,32]{0,1:T(8,128)(2,1)S(1)} fusion(bf16[640,6144]{1,0:T(8,128)(2,1)} %get-tuple-element.13, bf16[1,32,6144]{2,1,0:T(8,128)(2,1)} %param.18), kind=kOutput, calls=%fused_computation.24 | convolution fusion | flops 251678720 | bytes 8298496 | tf_op jit(solution)/shard_map/nd,rd->nr/dot_general | solution.py:16
  178.8 2.1 convolution_bitcast_fusion
  180.9 2.6 fusion.9
  183.6 0.3 fusion.13
  183.9 2.9 fusion.4
  186.8 0.3 fusion.11
  187.1 3.1 fusion.7
  190.2 0.6 multiply_reduce_fusion
  190.8 0.8 fusion.17
  191.6 0.2 fusion.14
  191.8 0.2 convolution_bitcast_fusion.2
  192.0 0.2 convolution_bitcast_fusion.1
  192.2 0.7 maximum_multiply_fusion
  192.9 0.2 fusion.15
  193.0 0.2 fusion.16
  193.2 0.7 pad_maximum_fusion
  193.9 26.3 %psum.7 = bf16[49,640]{1,0:T(8,128)(2,1)S(1)} all-reduce(bf16[49,640]{1,0:T(8,128)(2,1)} %pad_maximum_fusion), channel_id=1, replica_groups=mesh['dp'=4,'expert'=8] {'expert'}, use_global_device_ids=true, to_apply=%region_6.7 | all-reduce | flops 31360 | bytes 125440 | tf_op jit(solution)/shard_map/psum | solution.py:327
  220.2 5.1 %fusion.1 = f32[1,16,6144]{2,1,0:T(8,128)} fusion(bf16[640,6144]{1,0:T(8,128)(2,1)} %get-tuple-element.12, f32[640]{0:T(1024)S(1)} %reshape.142, bf16[49,640]{1,0:T(8,128)(2,1)S(1)} %psum.7), kind=kOutput, calls=%fused_computation.4 | convolution fusion | flops 125958144 | bytes 8282112 | tf_op jit(solution)/shard_map/rn,nd->rd/dot_general | solution.py:16
  225.3 5.6 %fusion = f32[1,32,6144]{2,1,0:T(8,128)} fusion(bf16[640,6144]{1,0:T(8,128)(2,1)} %get-tuple-element.13, bf16[49,640]{1,0:T(8,128)(2,1)S(1)} %psum.7), kind=kOutput, calls=%fused_computation.2 | convolution fusion | flops 251854848 | bytes 8691712 | tf_op jit(solution)/shard_map/rn,nd->rd/dot_general | solution.py:16
  230.9 0.6 broadcast_multiply_fusion
  231.5 0.8 mul.148
  232.2 0.6 fusion.58
  232.8 1.3 reshape.143
  234.2 0.7 add_convert_fusion.1
  234.9 1.2 convolution_multiply_fusion.2.extra
  236.2 7.8 %fusion.2 = f32[640,6144]{1,0:T(8,128)} fusion(bf16[640,256]{0,1:T(8,128)(2,1)S(1)} %get-tuple-element.20, bf16[1,6144,256]{2,1,0:T(8,128)(2,1)S(1)} %copy-done), kind=kOutput, calls=%fused_computation.5 | convolution fusion | flops 2013265920 | bytes 19202048 | tf_op jit(solution)/shard_map/nf,df->nd/dot_general | solution.py:16
  243.9 11.9 %add_convert_fusion.term = bf16[640,6144]{1,0:T(8,128)(2,1)} fusion(f32[640,6144]{1,0:T(8,128)} %fusion.2, bf16[640,256]{0,1:T(8,128)(2,1)S(1)} %copy-done.5, bf16[1,6144,256]{2,1,0:T(8,128)(2,1)} %param.16), kind=kOutput, calls=%fused_computation | convolution fusion | flops 2021130240 | bytes 27066368 | tf_op jit(solution)/shard_map/nf,df->nd/dot_general | solution.py:16
  255.9 3.2 copy-done.1
  259.1 96.4 %shard_map.155 = (bf16[640,768]{1,0:T(8,128)(2,1)S(1)}, bf16[4,16,256]{2,1,0:T(8,128)(2,1)S(1)}) custom-call(bf16[640,6144]{1,0:T(8,128)(2,1)S(1)} %copy-done.1, f32[640,768]{1,0:T(8,128)S(1)} %convolution_multiply_fusion.2.extra, bf16[4,16,256]{2,1,0:T(8,128)(2,1)S(1)} %broadcast_in_dim.75.gate_ref), custom_call_target="tpu_custom_call" | custom-call | tf_op jit(solution)/shard_map/pallas_call | solution.py:342
  355.5 1.3 convolution_convert_fusion.2
  356.9 0.3 select_reduce_fusion.1
  357.1 0.6 pad_maximum_fusion.1
  (46 shorter events, 0.5 us)
Async XLA Ops:
  0.6 183.3 %copy-start = (bf16[1,6144,256]{2,1,0:T(8,128)(2,1)S(1)}, bf16[1,6144,256]{2,1,0:T(8,128)(2,1)}, u32[]{:S(2)}) copy-start(bf16[1,6144,256]{2,1,0:T(8,128)(2,1)} %param.15) | copy-start | bytes 9437188
  0.6 178.1 %copy-start.8 = (bf16[1,16,6144]{2,1,0:T(8,128)(2,1)S(1)}, bf16[1,16,6144]{2,1,0:T(8,128)(2,1)}, u32[]{:S(2)}) copy-start(bf16[1,16,6144]{2,1,0:T(8,128)(2,1)} %param.21) | copy-start | bytes 589828
  5.5 175.4 %copy-start.11 = (s32[256,1]{0,1:T(1,128)}, s32[256,1]{0,1:T(1,128)S(1)}, u32[]{:S(2)}) copy-start(s32[256,1]{0,1:T(1,128)S(1)} %get-tuple-element.23) | copy-start | bytes 3076
  172.9 5.8 %copy-start.2 = (bf16[640,6144]{1,0:T(8,128)(2,1)S(1)}, bf16[640,6144]{1,0:T(8,128)(2,1)}, u32[]{:S(2)}) copy-start(bf16[640,6144]{1,0:T(8,128)(2,1)} %get-tuple-element.12) | copy-start | bytes 23592964
  172.9 8.0 %copy-start.13 = (bf16[1,256,6144]{2,1,0:T(8,128)(2,1)S(1)}, bf16[1,256,6144]{2,1,0:T(8,128)(2,1)}, u32[]{:S(2)}) copy-start(bf16[1,256,6144]{2,1,0:T(8,128)(2,1)} %param.17) | copy-start | bytes 9437188
  178.7 5.2 %slice-start = ((s8[7864320]{0:T(1024)(128)(4,1)}), s8[4194304]{0:T(1024)(128)(4,1)S(1)}, s32[]{:S(2)}) async-start(s8[7864320]{0:T(1024)(128)(4,1)} %bitcast.104), calls=%async_computation | async-start | bytes 8388608
  180.9 9.9 %copy-start.6 = (f32[16,640]{1,0:T(8,128)}, f32[16,640]{1,0:T(8,128)S(1)}, u32[]{:S(2)}) copy-start(f32[16,640]{1,0:T(8,128)S(1)} %convolution_bitcast_fusion) | copy-start | bytes 122884
  180.9 2.7 copy-start.10
  180.9 3.0 slice-start.1
  183.9 2.9 copy-start.9
  183.9 3.2 copy-start.3
  190.8 2.3 copy-start.4
  225.3 5.6 %copy-start.7 = (f32[16,640]{1,0:T(8,128)S(1)}, f32[16,640]{1,0:T(8,128)}, u32[]{:S(2)}) copy-start(f32[16,640]{1,0:T(8,128)} %copy-done.6) | copy-start | bytes 122884
  236.1 7.8 %copy-start.5 = (bf16[640,256]{0,1:T(8,128)(2,1)S(1)}, bf16[640,256]{0,1:T(8,128)(2,1)}, u32[]{:S(2)}) copy-start(bf16[640,256]{0,1:T(8,128)(2,1)} %copy-done.4) | copy-start | bytes 983044
  255.9 3.2 copy-start.1
  259.1 96.4 %copy-start.12 = (s32[256,1]{0,1:T(1,128)S(1)}, s32[256,1]{0,1:T(1,128)}, u32[]{:S(2)}) copy-start(s32[256,1]{0,1:T(1,128)} %copy-done.11) | copy-start | bytes 3076

commit v2 on v1

--- a/solution.py
+++ b/solution.py
@@ -131,8 +131,8 @@
     local[0].wait()
 
 
-def scatter_kernel(n, n_dp, cap, width, wide, term, extra, gate_ref, back, ogate,
-                   slots, final, local_sem, sent, came, ring_sent, ring_came):
+def scatter_kernel(n, n_dp, cap, width, gate_delta, up_delta, gate_weight, up_weight, extra,
+                   gate_ref, back, ogate, slots, final, own, stage, local_sem, sent, came, ring_sent, ring_came):
     me_dp, me_ex = lax.axis_index("dp"), lax.axis_index("expert")
     here = ring_position(me_ex, n)
     around = [ring_index(lax.rem(here + j, n), n) for j in range(n)]
@@ -144,11 +144,22 @@
             src_ref=src, dst_ref=dst, send_sem=send_sem, recv_sem=recv_sem,
             device_id=(dp, ex), device_id_type=MESH)
 
-    def own_part(row, group):
-        at = pl.ds(pl.multiple_of(row, tile_rows), tile_rows)
-        if wide:
-            return term[at, pl.ds(pl.multiple_of(group * width, 128), width)].astype(jnp.float32)
-        return term[group, at].astype(jnp.float32)
+    def form_terms(even_group, odd_group):
+        def piece(k, carry):
+            row = pl.multiple_of(lax.rem(me_dp + k, n_dp) * cap, tile_rows)
+            odd = lax.rem(k, 2)
+            group = (1 - odd) * even_group + odd * odd_group
+            rows_at = pl.ds(row, cap)
+            columns = pl.ds(pl.multiple_of(group * width, tile_rows), width)
+            dims = (((1,), (1,)), ((), ()))
+            own[rows_at] = lax.dot_general(
+                gate_delta[rows_at], gate_weight[columns], dims, preferred_element_type=jnp.float32
+            ) + lax.dot_general(
+                up_delta[rows_at], up_weight[columns], dims, preferred_element_type=jnp.float32
+            )
+            return carry
+
+        lax.fori_loop(0, n_dp, piece, 0)
 
     pending, arrivals = [], []
     for k in range(1, n_dp):
@@ -161,21 +172,28 @@
     own_gate.start()
     last = {}
     for s in range(n - 1):
+        form_terms(around[(n - 1 - s) % n], around[(1 + s) % n])
         for k in range(n_dp):
             row = lax.rem(me_dp + k, n_dp) * cap
             rows_at = pl.ds(pl.multiple_of(row, tile_rows), cap)
             forward = k % 2 == 0
-            group = around[(n - 1 - s) % n] if forward else around[(1 + s) % n]
             if s == 0:
-                src = block_view(term, row, cap, group, width, wide)
+                src = stage.at[rows_at]
+
+                def put(i, carry, row=row):
+                    at = pl.ds(pl.multiple_of(row + i * tile_rows, tile_rows), tile_rows)
+                    stage[at] = own[at].astype(jnp.bfloat16)
+                    return carry
+
+                lax.fori_loop(0, cap // tile_rows, put, 0)
             else:
                 last[k].wait_recv()
                 src = slots.at[s - 1, rows_at]
 
-                def add(i, carry, row=row, group=group, s=s):
+                def add(i, carry, row=row, s=s):
                     start = row + i * tile_rows
                     at = pl.ds(pl.multiple_of(start, tile_rows), tile_rows)
-                    total = slots[s - 1, at].astype(jnp.float32) + own_part(start, group)
+                    total = slots[s - 1, at].astype(jnp.float32) + own[at]
                     slots[s - 1, at] = total.astype(jnp.bfloat16)
                     return carry
 
@@ -185,6 +203,7 @@
             copy.start()
             last[k] = copy
             pending.append(copy)
+    form_terms(me_ex, me_ex)
     own_rows = None
     for k in list(range(1, n_dp)) + [0]:
         peer = lax.rem(me_dp + k, n_dp)
@@ -194,7 +213,7 @@
         def finish(i, carry, row=row):
             start = row + i * tile_rows
             at = pl.ds(pl.multiple_of(start, tile_rows), tile_rows)
-            total = slots[n - 2, at].astype(jnp.float32) + own_part(start, me_ex) + extra[at]
+            total = slots[n - 2, at].astype(jnp.float32) + own[at] + extra[at]
             final[at] = total.astype(jnp.bfloat16)
             return carry
 
@@ -329,26 +348,22 @@
     out_low = low_out.astype(f32)
     back_in = sums[low_rank : 3 * low_rank]
     gate_dots = sums[3 * low_rank].astype(f32) + adapter_scale * jnp.sum(out_low * back_low, axis=0)
-    term = (
-        product("nf,df->nd", gate_delta, gate_weight[0])
-        + product("nf,df->nd", up_delta, up_weight[0])
-    ).astype(bf16)
-    if not wide:
-        term = term.reshape(own_rows, n, width).transpose(1, 0, 2)
     shrink_cols = lax.dynamic_slice_in_dim(
         shrink_local, lax.axis_index("expert") * width, width, 1
     )
     extra = adapter_scale * product("rn,rd->nd", back_in, shrink_cols)
     token_back, gate_back = pl.pallas_call(
-        functools.partial(scatter_kernel, n, n_dp, cap, width, wide),
+        functools.partial(scatter_kernel, n, n_dp, cap, width),
         out_shape=(
             jax.ShapeDtypeStruct((own_rows, width), bf16),
             jax.ShapeDtypeStruct(gate_block.shape, bf16),
         ),
-        in_specs=[vmem] * 3,
+        in_specs=[vmem] * 6,
         out_specs=(anywhere,) * 2,
         scratch_shapes=[
             pltpu.VMEM((n - 1, own_rows, width), bf16),
+            pltpu.VMEM((own_rows, width), bf16),
+            pltpu.VMEM((own_rows, width), f32),
             pltpu.VMEM((own_rows, width), bf16),
             dma((2,)),
             dma((2, n_dp)),
@@ -359,7 +374,9 @@
         compiler_params=pltpu.CompilerParams(
             collective_id=1, has_side_effects=True, vmem_limit_bytes=40 * 1024 * 1024
         ),
-    )(term, extra, spread_rows(gate_dots, n_dp, cap))
+    )(
+        gate_delta, up_delta, gate_weight[0], up_weight[0], extra, spread_rows(gate_dots, n_dp, cap)
+    )
     token_grad = product("rt,rd->td", placing, token_back).astype(bf16)
     gate_flat = gate_back[:, 0, :cap].reshape(own_rows).astype(f32)
     gate_grad = jnp.stack(

time: 358 us -> 351 us (0.980)
  matrix products: 57.1 us -> 45.8 us
    dot_general x16 -> x14, matrix products: 45.5 us -> 32.1 us  [product(): jnp.einsum(pattern, operand_a, operand_b, preferred_element_type=jnp.floa...]
where the time goes in v2:
time: 351 us
  Pallas kernels  259 us (74%)
  matrix products  45.8 us (13%)
  blocking collectives  26.3 us (7%)
  local copies, waits for them, and re-layouts  11.6 us (3%)
  other arithmetic  7.25 us (2%)
    pallas_call x1, Pallas kernels, local(): pl.pallas_call(functools.partial(gather_kernel, n, n_dp, cap, width, wide...  161 us
    pallas_call x1, Pallas kernels, local(): pl.pallas_call(functools.partial(scatter_kernel, n, n_dp, cap, width), ou...  98 us
    dot_general x14, matrix products, product(): jnp.einsum(pattern, operand_a, operand_b, preferred_element_type=jnp.floa...  32.1 us
    psum x1, blocking collectives, local(): sums = lax.psum(parts, 'expert')  26.3 us
    unnamed x49, local copies, waits for them, and re-layouts  7.09 us

profile of v2, /device:TPU:5, one launch (start us, length us, event | category | flops | bytes accessed | tf_op | source)
XLA Modules:
  0.0 350.8 jit_solution(12781477269226980068)
XLA Ops:
  0.6 1.0 copy.53
  1.6 0.1 eq.59
  1.8 1.2 reduce-window.6
  3.0 0.2 slice_reduce_fusion
  3.2 0.2 reduce-window.9
  3.5 0.1 eq.55
  3.9 0.7 multiply_add_fusion
  4.6 0.8 fusion.58
  5.3 0.2 select_reduce_fusion.2
  5.7 0.6 broadcast_in_dim.73.gate_ref
  6.3 2.4 convolution_convert_fusion.dy_ref
  8.7 2.4 convolution_convert_fusion.1.x_ref
  11.1 160.8 %shard_map.154 = (bf16[640,6144]{1,0:T(8,128)(2,1)}, bf16[640,6144]{1,0:T(8,128)(2,1)}, bf16[4,16,256]{2,1,0:T(8,128)(2,1)}) custom-call(bf16[640,768]{1,0:T(8,128)(2,1)} %convolution_convert_fusion.1.x_ref, bf16[640,768]{1,0:T(8,128)(2,1)} %convolution_convert_fusion.dy_ref, bf16[4,16,256]{2,1,0:T(8,128)(2,1)} %broadcast_in_dim.73.gate_ref), custom_call_target="tpu_custom_call" | custom-call | tf_op jit(solution)/shard_map/pallas_call | solution.py:287
  172.0 5.5 %convolution_bitcast_fusion = f32[16,640]{1,0:T(8,128)S(1)} fusion(bf16[640,6144]{1,0:T(8,128)(2,1)} %get-tuple-element.12, bf16[1,16,6144]{2,1,0:T(8,128)(2,1)} %param.21), kind=kOutput, calls=%fused_computation.17 | convolution fusion | flops 125829120 | bytes 8101888 | tf_op jit(solution)/shard_map/rd,nd->rn/dot_general | solution.py:16
  177.5 3.1 fusion.2
  180.6 0.7 convert_reduce_fusion.1
  181.4 1.5 fusion.6
  183.0 5.8 %convolution_convert_fusion.3 = bf16[640,32]{0,1:T(8,128)(2,1)S(1)} fusion(bf16[640,6144]{1,0:T(8,128)(2,1)} %get-tuple-element.13, bf16[1,32,6144]{2,1,0:T(8,128)(2,1)} %param.18), kind=kOutput, calls=%fused_computation.16 | convolution fusion | flops 251678720 | bytes 8298496 | tf_op jit(solution)/shard_map/nd,rd->nr/dot_general | solution.py:16
  188.9 5.6 %fusion.53 = f32[640,256]{1,0:T(8,128)S(1)} fusion(bf16[640,6144]{1,0:T(8,128)(2,1)} %get-tuple-element.13, bf16[1,6144,256]{2,1,0:T(8,128)(2,1)S(1)} %copy-done.1), kind=kOutput, calls=%fused_computation.97 | convolution fusion | flops 2013265920 | bytes 11665408 | tf_op jit(solution)/shard_map/dot_general | solution.py:315
  194.5 0.3 fusion.4
  194.8 2.2 fusion.55
  197.0 0.8 multiply_reduce_fusion
  197.9 0.2 fusion.7
  198.0 0.2 fusion.8
  198.3 0.3 copy-done.5
  198.6 0.2 fusion.9
  198.8 0.6 pad_maximum_fusion
  199.4 26.3 %psum.7 = bf16[49,640]{1,0:T(8,128)(2,1)S(1)} all-reduce(bf16[49,640]{1,0:T(8,128)(2,1)} %pad_maximum_fusion), channel_id=1, replica_groups=mesh['dp'=4,'expert'=8] {'expert'}, use_global_device_ids=true, to_apply=%region_6.7 | all-reduce | flops 31360 | bytes 125440 | tf_op jit(solution)/shard_map/psum | solution.py:346
  225.8 5.2 %fusion.1 = f32[1,16,6144]{2,1,0:T(8,128)} fusion(bf16[640,6144]{1,0:T(8,128)(2,1)} %get-tuple-element.12, f32[640]{0:T(1024)S(1)} %reshape.142, bf16[49,640]{1,0:T(8,128)(2,1)S(1)} %psum.7), kind=kOutput, calls=%fused_computation.3 | convolution fusion | flops 125958144 | bytes 8282112 | tf_op jit(solution)/shard_map/rn,nd->rd/dot_general | solution.py:16
  231.0 0.8 fusion.10
  231.7 0.1 convolution_bitcast_fusion.2
  231.9 0.2 convolution_bitcast_fusion.1
  232.1 0.6 maximum_multiply_fusion
  232.7 5.6 %fusion = f32[1,32,6144]{2,1,0:T(8,128)} fusion(bf16[640,6144]{1,0:T(8,128)(2,1)} %get-tuple-element.13, bf16[49,640]{1,0:T(8,128)(2,1)S(1)} %psum.7), kind=kOutput, calls=%fused_computation.1 | convolution fusion | flops 251854848 | bytes 8691712 | tf_op jit(solution)/shard_map/rn,nd->rd/dot_general | solution.py:16
  238.3 0.6 broadcast_multiply_fusion
  238.9 1.3 mul.148
  240.2 0.6 fusion.51
  240.8 0.7 reshape.143
  241.6 0.7 add_convert_fusion
  242.3 1.3 convolution_multiply_fusion.2.extra
  243.6 1.9 copy-done.2
  245.5 1.9 copy-done.4
  247.4 1.0 copy-done.7
  248.3 98.0 %shard_map.155 = (bf16[640,768]{1,0:T(8,128)(2,1)S(1)}, bf16[4,16,256]{2,1,0:T(8,128)(2,1)S(1)}) custom-call(bf16[640,256]{1,0:T(8,128)(2,1)S(1)} %get-tuple-element.20.gate_delta, bf16[640,256]{1,0:T(8,128)(2,1)S(1)} %copy-done.7, bf16[6144,256]{1,0:T(8,128)(2,1)S(1)} %bitcast.98, bf16[6144,256]{1,0:T(8,128)(2,1)S(1)} %bitcast.99, ...), custom_call_target="tpu_custom_call" | custom-call | tf_op jit(solution)/shard_map/pallas_call | solution.py:355
  346.4 0.9 copy-done.8
  347.4 0.3 select_reduce_fusion.1
  347.7 0.6 pad_maximum_fusion.1
  348.3 2.5 convolution_convert_fusion.2
  (60 shorter events, 0.8 us)
Async XLA Ops:
  0.6 176.9 %copy-start = (bf16[1,256,6144]{2,1,0:T(8,128)(2,1)S(1)}, bf16[1,256,6144]{2,1,0:T(8,128)(2,1)}, u32[]{:S(2)}) copy-start(bf16[1,256,6144]{2,1,0:T(8,128)(2,1)} %param.17) | copy-start | bytes 9437188
  4.6 167.4 %copy-start.20 = (s32[256,1]{0,1:T(1,128)}, s32[256,1]{0,1:T(1,128)S(1)}, u32[]{:S(2)}) copy-start(s32[256,1]{0,1:T(1,128)S(1)} %get-tuple-element.23) | copy-start | bytes 3076
  172.0 5.5 %copy-start.9 = (bf16[640,6144]{1,0:T(8,128)(2,1)S(1)}, bf16[640,6144]{1,0:T(8,128)(2,1)}, u32[]{:S(2)}) copy-start(bf16[640,6144]{1,0:T(8,128)(2,1)} %get-tuple-element.12) | copy-start | bytes 23592964
  177.5 5.5 %copy-start.13 = (f32[16,640]{1,0:T(8,128)}, f32[16,640]{1,0:T(8,128)S(1)}, u32[]{:S(2)}) copy-start(f32[16,640]{1,0:T(8,128)S(1)} %convolution_bitcast_fusion) | copy-start | bytes 122884
  177.5 3.9 %copy-start.19 = (bf16[1,16,256]{2,1,0:T(8,128)(2,1)S(1)}, bf16[1,16,256]{2,1,0:T(8,128)(2,1)}, u32[]{:S(2)}) copy-start(bf16[1,16,256]{2,1,0:T(8,128)(2,1)} %param.20) | copy-start | bytes 24580
  181.4 7.4 %copy-start.1 = (bf16[1,6144,256]{2,1,0:T(8,128)(2,1)S(1)}, bf16[1,6144,256]{2,1,0:T(8,128)(2,1)}, u32[]{:S(2)}) copy-start(bf16[1,6144,256]{2,1,0:T(8,128)(2,1)} %param.15) | copy-start | bytes 9437188
  183.0 11.8 %slice-start = ((s8[7864320]{0:T(1024)(128)(4,1)}), s8[4194304]{0:T(1024)(128)(4,1)S(1)}, s32[]{:S(2)}) async-start(s8[7864320]{0:T(1024)(128)(4,1)} %bitcast.100), calls=%async_computation | async-start | bytes 8388608
  188.8 8.2 %copy-start.16 = (bf16[640,32]{0,1:T(8,128)(2,1)}, bf16[640,32]{0,1:T(8,128)(2,1)S(1)}, u32[]{:S(2)}) copy-start(bf16[640,32]{0,1:T(8,128)(2,1)S(1)} %convolution_convert_fusion.3) | copy-start | bytes 122884
  188.8 5.6 %copy-start.18 = (bf16[1,2,16,256]{3,2,1,0:T(8,128)(2,1)S(1)}, bf16[1,2,16,256]{3,2,1,0:T(8,128)(2,1)}, u32[]{:S(2)}) copy-start(bf16[1,2,16,256]{3,2,1,0:T(8,128)(2,1)} %param.19) | copy-start | bytes 49156
  188.8 6.0 %copy-start.3 = (bf16[1,6144,256]{2,1,0:T(8,128)(2,1)S(1)}, bf16[1,6144,256]{2,1,0:T(8,128)(2,1)}, u32[]{:S(2)}) copy-start(bf16[1,6144,256]{2,1,0:T(8,128)(2,1)} %param.16) | copy-start | bytes 9437188
  188.8 6.0 %slice-start.1 = ((s8[7864320]{0:T(1024)(128)(4,1)}), s8[3670016]{0:T(1024)(128)(4,1)S(1)}, s32[]{:S(2)}) async-start(s8[7864320]{0:T(1024)(128)(4,1)} %bitcast.100), calls=%async_computation.1 | async-start | bytes 7340032
  194.5 2.6 copy-start.15
  197.8 0.7 copy-start.5
  197.8 0.9 copy-start.10
  225.7 14.5 %copy-start.12 = (bf16[49,640]{1,0:T(8,128)(2,1)}, bf16[49,640]{1,0:T(8,128)(2,1)S(1)}, u32[]{:S(2)}) copy-start(bf16[49,640]{1,0:T(8,128)(2,1)S(1)} %psum.7) | copy-start | bytes 188164
  225.7 5.2 %copy-start.11 = (bf16[640,256]{1,0:T(8,128)(2,1)S(1)}, bf16[640,256]{1,0:T(8,128)(2,1)}, u32[]{:S(2)}) copy-start(bf16[640,256]{1,0:T(8,128)(2,1)} %copy-done.10) | copy-start | bytes 983044
  225.7 5.2 %copy-start.14 = (f32[16,640]{1,0:T(8,128)S(1)}, f32[16,640]{1,0:T(8,128)}, u32[]{:S(2)}) copy-start(f32[16,640]{1,0:T(8,128)} %copy-done.13) | copy-start | bytes 122884
  225.8 6.0 %copy-start.17 = (bf16[640,32]{0,1:T(8,128)(2,1)S(1)}, bf16[640,32]{0,1:T(8,128)(2,1)}, u32[]{:S(2)}) copy-start(bf16[640,32]{0,1:T(8,128)(2,1)} %copy-done.16) | copy-start | bytes 122884
  225.8 6.1 %copy-start.6 = (bf16[640,256]{1,0:T(8,128)(2,1)S(1)}, bf16[640,256]{1,0:T(8,128)(2,1)}, u32[]{:S(2)}) copy-start(bf16[640,256]{1,0:T(8,128)(2,1)} %copy-done.5) | copy-start | bytes 983044
  238.3 109.1 %copy-start.21 = (s32[256,1]{0,1:T(1,128)S(1)}, s32[256,1]{0,1:T(1,128)}, u32[]{:S(2)}) copy-start(s32[256,1]{0,1:T(1,128)} %copy-done.20) | copy-start | bytes 3076
  243.6 1.9 copy-start.2
  245.5 1.9 copy-start.4
  247.4 1.0 copy-start.7
  346.4 1.0 copy-start.8
